TPU v7x, 32 devices: a whole 2x2x4 slice. The times are simulated.
32 devices in a mesh: clip: 2 (over core), ha: 4 (over y, x), wa: 4 (over z).
Axes of the slice: x: 2, y: 2, z: 4, core: 2. Of those that a mesh axis runs over, the one named last changes fastest.
Arguments:
- frames: bfloat16 [8, 96, 128, 128], P('clip', 'ha', 'wa'), parts along dimension 0, may hold values from -60 to 60, as said below
- caches: bfloat16 [4, 4, 96, 128, 128], P('clip', None, 'ha', 'wa'), parts along dimension 0, may hold values from -4 to 4
- conv_weights: bfloat16 [4, 3, 3, 3, 128, 128], replicated, may hold values from -0.109375 to 0.109375
- conv_bias: float32 [4, 128], replicated, may hold values from -3 to 3
- norm_gain: float32 [4, 128], replicated, may hold values from 0.25 to 1.75
- norm_shift: float32 [4, 128], replicated, may hold values from -3 to 3
Outputs:
- encoded: bfloat16 [8, 96, 128, 128], P('clip', 'ha', 'wa'), parts along dimension 0
- new_caches: bfloat16 [4, 4, 96, 128, 128], P('clip', None, 'ha', 'wa'), parts along dimension 0
There are 2 independent parts, one for each index of `clip`. A program takes and returns all parts, laid end to end along the dimension named above; an argument that names none is the same for every part. Nothing has to cross between parts.
Inputs may be any that keep to these rules, and one draw needn't show every extreme that they name: `frames`: real-valued features.
All inputs are finite; a program needn't handle non-finite values.
Results may differ from a plain program's by a relative error of at most 0.005.
Values may be sent and summed in bfloat16 or wider, within the bound.
A program may use at most 64 MiB of HBM per device.

v0:
```python
import jax
import jax.numpy as jnp
from jax import lax
from jax.sharding import PartitionSpec as P

GROUPS = 32


EPSILON = 1e-06


def with_halo(cells, sides, width):
    for axis, dim in sides:
        count = lax.axis_size(axis)
        ends = count - 1
        head = lax.slice_in_dim(cells, 0, width, axis=dim)
        tail = lax.slice_in_dim(cells, cells.shape[dim] - width, cells.shape[dim], axis=dim)
        cells = jnp.concatenate(
            [
                lax.ppermute(tail, axis, [(i, (i + 1) % count) for i in range(ends)]),
                cells,
                lax.ppermute(head, axis, [((i + 1) % count, i) for i in range(ends)]),
            ],
            axis=dim,
        )
    return cells


def run_conv(padded, kernel, bias_row):
    result = lax.conv_general_dilated(
        padded[None],
        kernel,
        (1, 1, 1),
        "VALID",
        dimension_numbers=("NDHWC", "DHWIO", "NDHWC"),
        preferred_element_type=jnp.float32,
    )
    return result[0] + bias_row


def group_norm(values, interior, gain_row, shift_row, groups):
    channels = values.shape[-1]
    per_group = channels // groups
    cell_count = (
        interior.shape[0]
        * interior.shape[1]
        * interior.shape[2]
        * per_group
        * lax.axis_size("ha")
        * lax.axis_size("wa")
    )
    local_sums = jnp.sum(interior, axis=(0, 1, 2)).reshape(groups, per_group).sum(axis=1)
    local_squares = (
        jnp.sum(interior * interior, axis=(0, 1, 2)).reshape(groups, per_group).sum(axis=1)
    )
    group_total, squares = lax.psum((local_sums, local_squares), ("ha", "wa"))
    group_mean = group_total / cell_count
    variance = squares / cell_count - group_mean * group_mean
    reciprocal = lax.rsqrt(variance + EPSILON)
    multiplier = jnp.repeat(reciprocal, per_group) * gain_row
    offset = shift_row - jnp.repeat(group_mean * reciprocal, per_group) * gain_row
    return values * multiplier + offset


def causal_conv(activation, history, kernel, bias_row):
    joined = jnp.concatenate([history, activation], axis=0)
    padded = with_halo(joined, (("ha", 1), ("wa", 2)), 1)
    return run_conv(padded, kernel, bias_row)


def local(frames, caches, conv_weights, conv_bias, norm_gain, norm_shift):
    cache_frames = caches.shape[0]
    block_input = frames
    saved = []
    for block_index in range(conv_weights.shape[0] // 2):
        first_conv = 2 * block_index
        second_conv = first_conv + 1
        widened = block_input.astype(jnp.float32)
        first_act = jax.nn.silu(
            group_norm(widened, widened, norm_gain[first_conv], norm_shift[first_conv], GROUPS)
        ).astype(jnp.bfloat16)
        saved.append(first_act[first_act.shape[0] - cache_frames :])
        middle = causal_conv(
            first_act, caches[:, first_conv], conv_weights[first_conv], conv_bias[first_conv]
        )
        second_act = jax.nn.silu(
            group_norm(middle, middle, norm_gain[second_conv], norm_shift[second_conv], GROUPS)
        ).astype(jnp.bfloat16)
        saved.append(second_act[second_act.shape[0] - cache_frames :])
        branch = causal_conv(
            second_act, caches[:, second_conv], conv_weights[second_conv], conv_bias[second_conv]
        )
        block_input = (block_input.astype(jnp.float32) + branch).astype(jnp.bfloat16)
    return (block_input, jnp.stack(saved, axis=1))


def solution(mesh):
    return jax.shard_map(
        local,
        mesh=mesh,
        in_specs=(
            P("clip", "ha", "wa", None),
            P("clip", None, "ha", "wa", None),
            P(),
            P(),
            P(),
            P(),
        ),
        out_specs=(P("clip", "ha", "wa", None), P("clip", None, "ha", "wa", None)),
        check_vma=False,
    )
```

profile of v0, /device:TPU:0, one launch (start us, length us, event | category | flops | bytes accessed | tf_op | source)
XLA Modules:
  0.0 290.2 jit_solution(16235156809500017184)
XLA Ops:
  0.6 1.6 convert_reduce_fusion.1
  2.7 43.7 %all-reduce.3 = (f32[32]{0:T(128)S(1)}, f32[32]{0:T(128)S(1)}) all-reduce(f32[32]{0:T(128)S(1)} %reduce_sum.145, f32[32]{0:T(128)S(1)} %reduce_sum.147), channel_id=1, replica_groups=mesh['clip'=2,'ha'=4,'wa'=4] {'ha','wa'}, use_global_device_ids=true, to_apply=%region_2.0 | all-reduce | flops 64 | bytes 512 | tf_op jit(solution)/shard_map/psum | solution.py:56
  46.8 2.5 fusion.93
  55.3 4.8 %collective-permute-done.1 = bf16[6,1,32,128]{3,1,2,0:T(2,128)(2,1)S(1)} collective-permute-done((bf16[6,1,32,128]{3,1,2,0:T(2,128)(2,1)S(1)}, bf16[6,1,32,128]{3,1,2,0:T(2,128)(2,1)S(1)}, u32[]{:S(2)}, u32[]{:S(2)}) %collective-permute-start.1) | collective-permute-done | bytes 49184 | tf_op jit(solution)/shard_map/ppermute | solution.py:22
  61.4 1.8 collective-permute-start.3
  63.8 3.6 %collective-permute-done.3 = bf16[6,26,1,128]{3,1,2,0:T(8,128)(2,1)S(1)} collective-permute-done((bf16[6,26,1,128]{3,1,2,0:T(8,128)(2,1)S(1)}, bf16[6,26,1,128]{3,1,2,0:T(8,128)(2,1)S(1)}, u32[]{:S(2)}, u32[]{:S(2)}) %collective-permute-start.3) | collective-permute-done | bytes 39968 | tf_op jit(solution)/shard_map/ppermute | solution.py:22
  69.6 8.9 %fusion.63 = f32[4,24,8,5,128]{4,2,3,1,0:T(8,128)S(1)} fusion(bf16[6,26,1,7,2,128]{5,3,4,1,0,2:T(8,128)(2,1)S(1)} %slice.168, bf16[6,26,1,8,5,128]{5,3,4,1,0,2:T(8,128)(2,1)S(1)} %copy.19, pred[8,5]{0,1:T(8,128)(4,1)S(1)} %copy-done.12, bf16[4,3,3,3,128,128]{5,4,3,2,1,0:T(8,128)(2,1)} %param.8), kind=kOutput, calls=%fused_computation.75 | convolution fusion | flops 3404587008 | bytes 5007400 | tf_op jit(solution)/shard_map/conv_general_dilated | solution.py:30
  79.7 36.7 %all-reduce.2 = (f32[32]{0:T(128)S(1)}, f32[32]{0:T(128)S(1)}) all-reduce(f32[32]{0:T(128)S(1)} %reduce_sum.149, f32[32]{0:T(128)S(1)} %reduce_sum.151), channel_id=1, replica_groups=mesh['clip'=2,'ha'=4,'wa'=4] {'ha','wa'}, use_global_device_ids=true, to_apply=%region_8.9 | all-reduce | flops 64 | bytes 512 | tf_op jit(solution)/shard_map/psum | solution.py:56
  122.7 6.0 %collective-permute-done.5 = bf16[6,1,32,128]{3,1,2,0:T(2,128)(2,1)S(1)} collective-permute-done((bf16[6,1,32,128]{3,1,2,0:T(2,128)(2,1)S(1)}, bf16[6,1,32,128]{3,1,2,0:T(2,128)(2,1)S(1)}, u32[]{:S(2)}, u32[]{:S(2)}) %collective-permute-start.5) | collective-permute-done | bytes 49184 | tf_op jit(solution)/shard_map/ppermute | solution.py:22
  128.7 3.3 %collective-permute-start.6 = (bf16[6,26,1,128]{3,1,2,0:T(8,128)(2,1)S(1)}, bf16[6,26,1,128]{3,1,2,0:T(8,128)(2,1)S(1)}, u32[]{:S(2)}, u32[]{:S(2)}) collective-permute-start(bf16[6,26,1,128]{3,1,2,0:T(8,128)(2,1)S(1)} %get-tuple-element.37), channel_id=1, source_target_pairs={{0,1},{1,2},{2,3},{4,5},{5,6},{6,7},{8,9},{9,10},{10,11},{12,13},{... | collective-permute-start | bytes 119816 | tf_op jit(solution)/shard_map/ppermute | solution.py:20
  134.3 3.7 %collective-permute-done.7 = bf16[6,26,1,128]{3,1,2,0:T(8,128)(2,1)S(1)} collective-permute-done((bf16[6,26,1,128]{3,1,2,0:T(8,128)(2,1)S(1)}, bf16[6,26,1,128]{3,1,2,0:T(8,128)(2,1)S(1)}, u32[]{:S(2)}, u32[]{:S(2)}) %collective-permute-start.7) | collective-permute-done | bytes 39968 | tf_op jit(solution)/shard_map/ppermute | solution.py:22
  140.2 8.9 %fusion.60 = f32[4,24,8,5,128]{4,2,3,1,0:T(8,128)S(1)} fusion(bf16[6,26,1,7,2,128]{5,3,4,1,0,2:T(8,128)(2,1)S(1)} %slice.170, bf16[6,26,1,8,5,128]{5,3,4,1,0,2:T(8,128)(2,1)S(1)} %copy.22, pred[8,5]{0,1:T(8,128)(4,1)S(1)} %copy-done.13, bf16[4,3,3,3,128,128]{5,4,3,2,1,0:T(8,128)(2,1)} %param.8), kind=kOutput, calls=%fused_computation.74 | convolution fusion | flops 3404587008 | bytes 5007400 | tf_op jit(solution)/shard_map/conv_general_dilated | solution.py:30
  151.1 36.7 %all-reduce.1 = (f32[32]{0:T(128)S(1)}, f32[32]{0:T(128)S(1)}) all-reduce(f32[32]{0:T(128)S(1)} %reduce_sum.153, f32[32]{0:T(128)S(1)} %reduce_sum.155), channel_id=1, replica_groups=mesh['clip'=2,'ha'=4,'wa'=4] {'ha','wa'}, use_global_device_ids=true, to_apply=%region_14.15 | all-reduce | flops 64 | bytes 512 | tf_op jit(solution)/shard_map/psum | solution.py:56
  192.5 5.6 %collective-permute-done.9 = bf16[6,1,32,128]{3,1,2,0:T(2,128)(2,1)S(1)} collective-permute-done((bf16[6,1,32,128]{3,1,2,0:T(2,128)(2,1)S(1)}, bf16[6,1,32,128]{3,1,2,0:T(2,128)(2,1)S(1)}, u32[]{:S(2)}, u32[]{:S(2)}) %collective-permute-start.9) | collective-permute-done | bytes 49184 | tf_op jit(solution)/shard_map/ppermute | solution.py:22
  198.1 3.7 %collective-permute-start.10 = (bf16[6,26,1,128]{3,1,2,0:T(8,128)(2,1)S(1)}, bf16[6,26,1,128]{3,1,2,0:T(8,128)(2,1)S(1)}, u32[]{:S(2)}, u32[]{:S(2)}) collective-permute-start(bf16[6,26,1,128]{3,1,2,0:T(8,128)(2,1)S(1)} %get-tuple-element.35), channel_id=1, source_target_pairs={{0,1},{1,2},{2,3},{4,5},{5,6},{6,7},{8,9},{9,10},{10,11},{12,13},{... | collective-permute-start | bytes 119816 | tf_op jit(solution)/shard_map/ppermute | solution.py:20
  201.8 1.5 collective-permute-start.11
  204.1 3.7 %collective-permute-done.11 = bf16[6,26,1,128]{3,1,2,0:T(8,128)(2,1)S(1)} collective-permute-done((bf16[6,26,1,128]{3,1,2,0:T(8,128)(2,1)S(1)}, bf16[6,26,1,128]{3,1,2,0:T(8,128)(2,1)S(1)}, u32[]{:S(2)}, u32[]{:S(2)}) %collective-permute-start.11) | collective-permute-done | bytes 39968 | tf_op jit(solution)/shard_map/ppermute | solution.py:22
  209.9 8.9 %fusion.57 = f32[4,24,8,5,128]{4,2,3,1,0:T(8,128)S(1)} fusion(bf16[6,26,1,7,2,128]{5,3,4,1,0,2:T(8,128)(2,1)S(1)} %slice.172, bf16[6,26,1,8,5,128]{5,3,4,1,0,2:T(8,128)(2,1)S(1)} %copy.27, pred[8,5]{0,1:T(8,128)(4,1)S(1)} %copy-done.13, bf16[4,3,3,3,128,128]{5,4,3,2,1,0:T(8,128)(2,1)} %param.8), kind=kOutput, calls=%fused_computation.73 | convolution fusion | flops 3404587008 | bytes 5007400 | tf_op jit(solution)/shard_map/conv_general_dilated | solution.py:30
  220.0 36.8 %all-reduce = (f32[32]{0:T(128)S(1)}, f32[32]{0:T(128)S(1)}) all-reduce(f32[32]{0:T(128)S(1)} %reduce_sum.157, f32[32]{0:T(128)S(1)} %reduce_sum.159), channel_id=1, replica_groups=mesh['clip'=2,'ha'=4,'wa'=4] {'ha','wa'}, use_global_device_ids=true, to_apply=%region_20.21 | all-reduce | flops 64 | bytes 512 | tf_op jit(solution)/shard_map/psum | solution.py:56
  261.6 5.6 %collective-permute-done.13 = bf16[6,1,32,128]{3,1,2,0:T(2,128)(2,1)S(1)} collective-permute-done((bf16[6,1,32,128]{3,1,2,0:T(2,128)(2,1)S(1)}, bf16[6,1,32,128]{3,1,2,0:T(2,128)(2,1)S(1)}, u32[]{:S(2)}, u32[]{:S(2)}) %collective-permute-start.13) | collective-permute-done | bytes 49184 | tf_op jit(solution)/shard_map/ppermute | solution.py:22
  267.3 3.7 %collective-permute-start.14 = (bf16[6,26,1,128]{3,1,2,0:T(8,128)(2,1)S(1)}, bf16[6,26,1,128]{3,1,2,0:T(8,128)(2,1)S(1)}, u32[]{:S(2)}, u32[]{:S(2)}) collective-permute-start(bf16[6,26,1,128]{3,1,2,0:T(8,128)(2,1)S(1)} %get-tuple-element.33), channel_id=1, source_target_pairs={{0,1},{1,2},{2,3},{4,5},{5,6},{6,7},{8,9},{9,10},{10,11},{12,13},{... | collective-permute-start | bytes 119816 | tf_op jit(solution)/shard_map/ppermute | solution.py:20
  271.0 1.5 collective-permute-start.15
  274.2 2.7 collective-permute-done.15
  279.1 8.9 %fusion.54 = f32[4,24,8,5,128]{4,2,3,1,0:T(8,128)S(1)} fusion(bf16[6,26,1,7,2,128]{5,3,4,1,0,2:T(8,128)(2,1)S(1)} %slice.174, bf16[6,26,1,8,5,128]{5,3,4,1,0,2:T(8,128)(2,1)S(1)} %copy.30, pred[8,5]{0,1:T(8,128)(4,1)S(1)} %copy-done.14, bf16[4,3,3,3,128,128]{5,4,3,2,1,0:T(8,128)(2,1)} %param.8), kind=kOutput, calls=%fused_computation.72 | convolution fusion | flops 3404587008 | bytes 5007400 | tf_op jit(solution)/shard_map/conv_general_dilated | solution.py:30
  (134 shorter events, 43.5 us)
Async XLA Ops:
  2.2 47.1 %copy-start.9 = (f32[4,128]{1,0:T(4,128)S(1)}, f32[4,128]{1,0:T(4,128)}, u32[]{:S(2)}) copy-start(f32[4,128]{1,0:T(4,128)} %param.10) | copy-start | bytes 6148
  2.2 47.8 %copy-start = (bf16[4,24,32,128]{3,2,1,0:T(8,128)(2,1)S(1)}, bf16[4,24,32,128]{3,2,1,0:T(8,128)(2,1)}, u32[]{:S(2)}) copy-start(bf16[4,24,32,128]{3,2,1,0:T(8,128)(2,1)} %param.6) | copy-start | bytes 2359300
  51.6 11.6 %copy-start.8 = (f32[4,128]{1,0:T(4,128)S(1)}, f32[4,128]{1,0:T(4,128)}, u32[]{:S(2)}) copy-start(f32[4,128]{1,0:T(4,128)} %param.9) | copy-start | bytes 6148
  51.8 3.5 %collective-permute-start = (bf16[6,1,32,128]{3,1,2,0:T(2,128)(2,1)S(1)}, bf16[6,1,32,128]{3,1,2,0:T(2,128)(2,1)S(1)}, u32[]{:S(2)}, u32[]{:S(2)}) collective-permute-start(bf16[6,1,32,128]{3,1,2,0:T(2,128)(2,1)S(1)} %get-tuple-element.47), channel_id=1, source_target_pairs={{0,4},{4,8},{8,12},{1,5},{5,9},{9,13},{2,6},{6,10},{10,14},{3,7},{... | collective-permute-start | bytes 147464 | tf_op jit(solution)/shard_map/ppermute | solution.py:20
  53.1 7.0 %collective-permute-start.1 = (bf16[6,1,32,128]{3,1,2,0:T(2,128)(2,1)S(1)}, bf16[6,1,32,128]{3,1,2,0:T(2,128)(2,1)S(1)}, u32[]{:S(2)}, u32[]{:S(2)}) collective-permute-start(bf16[6,1,32,128]{3,1,2,0:T(2,128)(2,1)S(1)} %get-tuple-element.48), channel_id=1, source_target_pairs={{4,0},{8,4},{12,8},{5,1},{9,5},{13,9},{6,2},{10,6},{14,10},{7,3},{... | collective-permute-start | bytes 147464 | tf_op jit(solution)/shard_map/ppermute | solution.py:22
  60.1 3.7 %collective-permute-start.2 = (bf16[6,26,1,128]{3,1,2,0:T(8,128)(2,1)S(1)}, bf16[6,26,1,128]{3,1,2,0:T(8,128)(2,1)S(1)}, u32[]{:S(2)}, u32[]{:S(2)}) collective-permute-start(bf16[6,26,1,128]{3,1,2,0:T(8,128)(2,1)S(1)} %get-tuple-element.39), channel_id=1, source_target_pairs={{0,1},{1,2},{2,3},{4,5},{5,6},{6,7},{8,9},{9,10},{10,11},{12,13},{... | collective-permute-start | bytes 119816 | tf_op jit(solution)/shard_map/ppermute | solution.py:20
  61.4 6.0 %collective-permute-start.3 = (bf16[6,26,1,128]{3,1,2,0:T(8,128)(2,1)S(1)}, bf16[6,26,1,128]{3,1,2,0:T(8,128)(2,1)S(1)}, u32[]{:S(2)}, u32[]{:S(2)}) collective-permute-start(bf16[6,26,1,128]{3,1,2,0:T(8,128)(2,1)S(1)} %get-tuple-element.40), channel_id=1, source_target_pairs={{1,0},{2,1},{3,2},{5,4},{6,5},{7,6},{9,8},{10,9},{11,10},{13,12},{... | collective-permute-start | bytes 119816 | tf_op jit(solution)/shard_map/ppermute | solution.py:22
  118.0 10.7 %copy-start.2 = (bf16[2,24,32,128]{3,1,2,0:T(8,128)(2,1)S(1)}, bf16[2,24,32,128]{3,1,2,0:T(8,128)(2,1)}, u32[]{:S(2)}) copy-start(bf16[2,24,32,128]{3,1,2,0:T(8,128)(2,1)} %get-tuple-element.64) | copy-start | bytes 1179652
  119.2 3.5 %collective-permute-start.4 = (bf16[6,1,32,128]{3,1,2,0:T(2,128)(2,1)S(1)}, bf16[6,1,32,128]{3,1,2,0:T(2,128)(2,1)S(1)}, u32[]{:S(2)}, u32[]{:S(2)}) collective-permute-start(bf16[6,1,32,128]{3,1,2,0:T(2,128)(2,1)S(1)} %get-tuple-element.45), channel_id=1, source_target_pairs={{0,4},{4,8},{8,12},{1,5},{5,9},{9,13},{2,6},{6,10},{10,14},{3,7},{... | collective-permute-start | bytes 147464 | tf_op jit(solution)/shard_map/ppermute | solution.py:20
  120.5 8.2 %collective-permute-start.5 = (bf16[6,1,32,128]{3,1,2,0:T(2,128)(2,1)S(1)}, bf16[6,1,32,128]{3,1,2,0:T(2,128)(2,1)S(1)}, u32[]{:S(2)}, u32[]{:S(2)}) collective-permute-start(bf16[6,1,32,128]{3,1,2,0:T(2,128)(2,1)S(1)} %get-tuple-element.46), channel_id=1, source_target_pairs={{4,0},{8,4},{12,8},{5,1},{9,5},{13,9},{6,2},{10,6},{14,10},{7,3},{... | collective-permute-start | bytes 147464 | tf_op jit(solution)/shard_map/ppermute | solution.py:22
  128.7 5.6 %collective-permute-start.6 = (bf16[6,26,1,128]{3,1,2,0:T(8,128)(2,1)S(1)}, bf16[6,26,1,128]{3,1,2,0:T(8,128)(2,1)S(1)}, u32[]{:S(2)}, u32[]{:S(2)}) collective-permute-start(bf16[6,26,1,128]{3,1,2,0:T(8,128)(2,1)S(1)} %get-tuple-element.37), channel_id=1, source_target_pairs={{0,1},{1,2},{2,3},{4,5},{5,6},{6,7},{8,9},{9,10},{10,11},{12,13},{... | collective-permute-start | bytes 119816 | tf_op jit(solution)/shard_map/ppermute | solution.py:20
  132.1 6.0 %collective-permute-start.7 = (bf16[6,26,1,128]{3,1,2,0:T(8,128)(2,1)S(1)}, bf16[6,26,1,128]{3,1,2,0:T(8,128)(2,1)S(1)}, u32[]{:S(2)}, u32[]{:S(2)}) collective-permute-start(bf16[6,26,1,128]{3,1,2,0:T(8,128)(2,1)S(1)} %get-tuple-element.38), channel_id=1, source_target_pairs={{1,0},{2,1},{3,2},{5,4},{6,5},{7,6},{9,8},{10,9},{11,10},{13,12},{... | collective-permute-start | bytes 119816 | tf_op jit(solution)/shard_map/ppermute | solution.py:22
  149.5 38.8 %copy-start.10 = (f32[4,128]{1,0:T(4,128)S(1)}, f32[4,128]{1,0:T(4,128)}, u32[]{:S(2)}) copy-start(f32[4,128]{1,0:T(4,128)} %param.11) | copy-start | bytes 6148
  188.9 3.5 %collective-permute-start.8 = (bf16[6,1,32,128]{3,1,2,0:T(2,128)(2,1)S(1)}, bf16[6,1,32,128]{3,1,2,0:T(2,128)(2,1)S(1)}, u32[]{:S(2)}, u32[]{:S(2)}) collective-permute-start(bf16[6,1,32,128]{3,1,2,0:T(2,128)(2,1)S(1)} %get-tuple-element.43), channel_id=1, source_target_pairs={{0,4},{4,8},{8,12},{1,5},{5,9},{9,13},{2,6},{6,10},{10,14},{3,7},{... | collective-permute-start | bytes 147464 | tf_op jit(solution)/shard_map/ppermute | solution.py:20
  190.3 7.8 %collective-permute-start.9 = (bf16[6,1,32,128]{3,1,2,0:T(2,128)(2,1)S(1)}, bf16[6,1,32,128]{3,1,2,0:T(2,128)(2,1)S(1)}, u32[]{:S(2)}, u32[]{:S(2)}) collective-permute-start(bf16[6,1,32,128]{3,1,2,0:T(2,128)(2,1)S(1)} %get-tuple-element.44), channel_id=1, source_target_pairs={{4,0},{8,4},{12,8},{5,1},{9,5},{13,9},{6,2},{10,6},{14,10},{7,3},{... | collective-permute-start | bytes 147464 | tf_op jit(solution)/shard_map/ppermute | solution.py:22
  198.1 6.0 %collective-permute-start.10 = (bf16[6,26,1,128]{3,1,2,0:T(8,128)(2,1)S(1)}, bf16[6,26,1,128]{3,1,2,0:T(8,128)(2,1)S(1)}, u32[]{:S(2)}, u32[]{:S(2)}) collective-permute-start(bf16[6,26,1,128]{3,1,2,0:T(8,128)(2,1)S(1)} %get-tuple-element.35), channel_id=1, source_target_pairs={{0,1},{1,2},{2,3},{4,5},{5,6},{6,7},{8,9},{9,10},{10,11},{12,13},{... | collective-permute-start | bytes 119816 | tf_op jit(solution)/shard_map/ppermute | solution.py:20
  201.8 6.0 %collective-permute-start.11 = (bf16[6,26,1,128]{3,1,2,0:T(8,128)(2,1)S(1)}, bf16[6,26,1,128]{3,1,2,0:T(8,128)(2,1)S(1)}, u32[]{:S(2)}, u32[]{:S(2)}) collective-permute-start(bf16[6,26,1,128]{3,1,2,0:T(8,128)(2,1)S(1)} %get-tuple-element.36), channel_id=1, source_target_pairs={{1,0},{2,1},{3,2},{5,4},{6,5},{7,6},{9,8},{10,9},{11,10},{13,12},{... | collective-permute-start | bytes 119816 | tf_op jit(solution)/shard_map/ppermute | solution.py:22
  257.8 14.8 %copy-start.3 = (bf16[2,1,24,32,128]{4,2,3,0,1:T(8,128)(2,1)S(1)}, bf16[2,1,24,32,128]{4,2,3,0,1:T(8,128)(2,1)}, u32[]{:S(2)}) copy-start(bf16[2,1,24,32,128]{4,2,3,0,1:T(8,128)(2,1)} %slice_bitcast_fusion.7) | copy-start | bytes 1179652
  257.8 14.8 %copy-start.6 = (bf16[2,1,24,32,128]{4,2,3,0,1:T(8,128)(2,1)S(1)}, bf16[2,1,24,32,128]{4,2,3,0,1:T(8,128)(2,1)}, u32[]{:S(2)}) copy-start(bf16[2,1,24,32,128]{4,2,3,0,1:T(8,128)(2,1)} %slice_bitcast_fusion.6) | copy-start | bytes 1179652
  257.8 14.8 %copy-start.7 = (bf16[2,1,24,32,128]{4,2,3,0,1:T(8,128)(2,1)S(1)}, bf16[2,1,24,32,128]{4,2,3,0,1:T(8,128)(2,1)}, u32[]{:S(2)}) copy-start(bf16[2,1,24,32,128]{4,2,3,0,1:T(8,128)(2,1)} %slice_bitcast_fusion.5) | copy-start | bytes 1179652
  258.0 3.6 %collective-permute-start.12 = (bf16[6,1,32,128]{3,1,2,0:T(2,128)(2,1)S(1)}, bf16[6,1,32,128]{3,1,2,0:T(2,128)(2,1)S(1)}, u32[]{:S(2)}, u32[]{:S(2)}) collective-permute-start(bf16[6,1,32,128]{3,1,2,0:T(2,128)(2,1)S(1)} %get-tuple-element.41), channel_id=1, source_target_pairs={{0,4},{4,8},{8,12},{1,5},{5,9},{9,13},{2,6},{6,10},{10,14},{3,7},{... | collective-permute-start | bytes 147464 | tf_op jit(solution)/shard_map/ppermute | solution.py:20
  259.4 7.8 %collective-permute-start.13 = (bf16[6,1,32,128]{3,1,2,0:T(2,128)(2,1)S(1)}, bf16[6,1,32,128]{3,1,2,0:T(2,128)(2,1)S(1)}, u32[]{:S(2)}, u32[]{:S(2)}) collective-permute-start(bf16[6,1,32,128]{3,1,2,0:T(2,128)(2,1)S(1)} %get-tuple-element.42), channel_id=1, source_target_pairs={{4,0},{8,4},{12,8},{5,1},{9,5},{13,9},{6,2},{10,6},{14,10},{7,3},{... | collective-permute-start | bytes 147464 | tf_op jit(solution)/shard_map/ppermute | solution.py:22
  267.3 7.0 %collective-permute-start.14 = (bf16[6,26,1,128]{3,1,2,0:T(8,128)(2,1)S(1)}, bf16[6,26,1,128]{3,1,2,0:T(8,128)(2,1)S(1)}, u32[]{:S(2)}, u32[]{:S(2)}) collective-permute-start(bf16[6,26,1,128]{3,1,2,0:T(8,128)(2,1)S(1)} %get-tuple-element.33), channel_id=1, source_target_pairs={{0,1},{1,2},{2,3},{4,5},{5,6},{6,7},{8,9},{9,10},{10,11},{12,13},{... | collective-permute-start | bytes 119816 | tf_op jit(solution)/shard_map/ppermute | solution.py:20
  271.0 6.0 %collective-permute-start.15 = (bf16[6,26,1,128]{3,1,2,0:T(8,128)(2,1)S(1)}, bf16[6,26,1,128]{3,1,2,0:T(8,128)(2,1)S(1)}, u32[]{:S(2)}, u32[]{:S(2)}) collective-permute-start(bf16[6,26,1,128]{3,1,2,0:T(8,128)(2,1)S(1)} %get-tuple-element.34), channel_id=1, source_target_pairs={{1,0},{2,1},{3,2},{5,4},{6,5},{7,6},{9,8},{10,9},{11,10},{13,12},{... | collective-permute-start | bytes 119816 | tf_op jit(solution)/shard_map/ppermute | solution.py:22
  (7 other events, 12.9 us)
where the time goes:
time: 294 us; the launch traced here: 290 us
  blocking collectives  154 us (52%)
  waiting for transfers between devices  38.2 us (13%)
  matrix products  35.6 us (12%)
  starting transfers between devices  28.9 us (10%)
  local copies, waits for them, and re-layouts  18.7 us (6%)
  other arithmetic  13.2 us (4%)
    psum x4, blocking collectives, group_norm(): group_total, squares = lax.psum((local_sums, local_squares), ('ha', 'wa'))  154 us
    ppermute x8, waiting for transfers between devices, with_halo(): lax.ppermute(head, axis, [((i + 1) % count, i) for i in range(ends)])  35.8 us
    conv_general_dilated x4, matrix products, run_conv(): lax.conv_general_dilated(padded[None], kernel, (1, 1, 1), 'VALID', dimens...  35.6 us
    ppermute x8, starting transfers between devices, with_halo(): lax.ppermute(tail, axis, [(i, (i + 1) % count) for i in range(ends)])  17.4 us
    ppermute x8, starting transfers between devices, with_halo(): lax.ppermute(head, axis, [((i + 1) % count, i) for i in range(ends)])  11.4 us
  transfers between devices with their start and end apart: 16, of which 12 were waited for; matrix products, arithmetic and copies ran while one was open for 2% of the time, Pallas kernels for 0%

commit v1 on v0

v1 whole, which is shorter than its diff:
```python
import functools

import jax
import jax.numpy as jnp
from jax import lax
from jax.experimental import pallas as pl
from jax.experimental.pallas import tpu as pltpu
from jax.sharding import PartitionSpec as P

GROUPS = 32
EPSILON = 1e-06
MESH = pl.DeviceIdType.MESH
F32 = jnp.float32
BF16 = jnp.bfloat16
ROW_BLOCK = 8
DIRECTIONS = [(dy, dx) for dy in (-1, 0, 1) for dx in (-1, 0, 1) if (dy, dx) != (0, 0)]


def kernel(dims, *refs):
    (frames, caches, weights, bias, gain, shift, encoded, kept,
     x, cb, v, vc, a, t, acc, y,
     s_out, s_in,
     lc_out, lk_out, lr_in, lc_in, lk_in,
     cc_out, ck_out, cr_in, cc_in, ck_in,
     load_sem, weight_sem, kept_sem, out_sem,
     stat_send, stat_recv, halo_send, halo_recv) = refs
    nh, nw, fr, cf, convs, h, w, c = dims
    pitch = w + 8
    peers = nh * nw
    cell_count = fr * h * w * peers * (c // GROUPS)
    clip, ha, wa = lax.axis_index("clip"), lax.axis_index("ha"), lax.axis_index("wa")
    me = ha * nw + wa
    others = [
        (lax.rem(ha + i, nh), lax.rem(wa + j, nw))
        for i in range(nh)
        for j in range(nw)
        if (i, j) != (0, 0)
    ]
    barrier = pltpu.get_barrier_semaphore()
    for ph, pw in others:
        pl.semaphore_signal(barrier, inc=1, device_id=(clip, ph, pw), device_id_type=MESH)

    load_x = pltpu.make_async_copy(frames, x, load_sem.at[0])
    load_x.start()
    load_c = pltpu.make_async_copy(caches, cb, load_sem.at[1])
    load_c.start()

    def weight_copies(k):
        copies = []
        for dt in range(3):
            for half in range(2):
                copies.append(
                    pltpu.make_async_copy(
                        weights.at[k, dt],
                        t.at[k, dt + half, :, :, pl.ds(half * c, c)],
                        weight_sem.at[k, dt * 2 + half],
                    )
                )
        return copies

    for k in range(convs):
        for copy in weight_copies(k):
            copy.start()

    def zero_weights(k, carry):
        t[k, 3, :, :, 0:c] = jnp.zeros((3, 3 * c, c), BF16)
        t[k, 0, :, :, c : 2 * c] = jnp.zeros((3, 3 * c, c), BF16)
        return carry

    lax.fori_loop(0, convs, zero_weights, 0)

    def exists(dy, dx):
        conds = []
        if dy:
            conds.append(ha > 0 if dy < 0 else ha < nh - 1)
        if dx:
            conds.append(wa > 0 if dx < 0 else wa < nw - 1)
        return conds[0] if len(conds) == 1 else jnp.logical_and(*conds)

    def halo_copy(live, k, dy, dx, towards):
        e = k if live else convs + k
        field = v if live else vc.at[k]
        rows_in = lr_in if live else cr_in
        cols_out, cols_in = (lc_out, lc_in) if live else (cc_out, cc_in)
        ends_out, ends_in = (lk_out, lk_in) if live else (ck_out, ck_in)
        if dx == 0:
            src = field.at[:, pl.ds(0 if dy < 0 else (h - 1) * w, w), :]
            dst = rows_in.at[k, int(dy < 0)]
        elif dy == 0:
            src = cols_out.at[k, int(dx > 0)]
            dst = cols_in.at[k, int(dx < 0)]
        else:
            index = int(dy > 0) * 2 + int(dx > 0)
            src = ends_out.at[k, index]
            dst = ends_in.at[k, 3 - index]
        d = DIRECTIONS.index((dy, dx))
        back = DIRECTIONS.index((-dy, -dx))
        return pltpu.make_async_remote_copy(
            src_ref=src,
            dst_ref=dst,
            send_sem=halo_send.at[e, d],
            recv_sem=halo_recv.at[e, back],
            device_id=(clip, ha + dy * towards, wa + dx * towards),
            device_id_type=MESH,
        )

    def pack_edges(live, k):
        field = v if live else vc.at[k]
        cols_out = lc_out if live else cc_out
        ends_out = lk_out if live else ck_out
        for f in range(fr if live else cf):
            for side in range(2):
                first = side * (w - 1)
                cols_out[k, side, f] = field[f, pl.ds(first, h, stride=w), :]
                for low in range(2):
                    row = low * (h - 1) * w + first
                    ends_out[k, low * 2 + side, f] = field[f, row : row + 1, :]

    def send_halo(live, k):
        pack_edges(live, k)
        for dy, dx in DIRECTIONS:

            @pl.when(exists(dy, dx))
            def _():
                halo_copy(live, k, dy, dx, 1).start()

    def wait_halo(live, k):
        for dy, dx in DIRECTIONS:

            @pl.when(exists(dy, dx))
            def _():
                halo_copy(live, k, -dy, -dx, -1).wait_recv()

    def wait_sent(live, k):
        for dy, dx in DIRECTIONS:

            @pl.when(exists(dy, dx))
            def _():
                halo_copy(live, k, dy, dx, 1).wait_send()

    def stat_copy(k, number, sender):
        ph, pw = others[number]
        return pltpu.make_async_remote_copy(
            src_ref=s_out.at[k],
            dst_ref=s_in.at[k, sender],
            send_sem=stat_send.at[k, number],
            recv_sem=stat_recv.at[k, sender],
            device_id=(clip, ph, pw),
            device_id_type=MESH,
        )

    def send_stats(k, sums, squares):
        both = jnp.concatenate(
            [jnp.sum(sums, axis=0, keepdims=True), jnp.sum(squares, axis=0, keepdims=True)], axis=0
        )
        s_out[k] = both
        s_in[k, me] = both
        for number in range(peers - 1):
            stat_copy(k, number, me).start()

    def wait_stats(k):
        for number, (ph, pw) in enumerate(others):
            stat_copy(k, number, ph * nw + pw).wait_recv()
        total = s_in[k, 0]
        for i in range(1, peers):
            total = total + s_in[k, i]
        total = jnp.concatenate([total, jnp.zeros((6, c), F32)], axis=0)
        lane = lax.broadcasted_iota(jnp.int32, (8, c), 1)
        step = 1
        while step < c // GROUPS:
            total = total + jnp.where(
                lax.rem(lane, 2 * step) < step,
                pltpu.roll(total, c - step, 1),
                pltpu.roll(total, step, 1),
            )
            step *= 2
        mean = total[0:1] / cell_count
        variance = total[1:2] / cell_count - mean * mean
        multiplier = lax.rsqrt(variance + EPSILON) * gain[k : k + 1, :]
        offset = shift[k : k + 1, :] - mean * multiplier
        return multiplier, offset

    def silu(values):
        half = 0.5 * values
        return half + half * jnp.tanh(half)

    def build(par, f, row_of, rows, cols, ends):
        for r in range(h + 2):
            cells = rows[0]() if r == 0 else rows[1]() if r == h + 1 else row_of(r - 1)
            a[par, f, r, :, c : 2 * c] = cells.astype(BF16)
            y[r * pitch + 1 : r * pitch + 1 + w, :] = cells
        for side in range(2):
            edge = side * (w + 1)
            y[pl.ds(pitch + edge, h, stride=pitch), :] = cols[side]()
            for low in range(2):
                at = low * (h + 1) * pitch + edge
                y[at : at + 1, :] = ends[low * 2 + side]()
        for r in range(h + 2):
            for dw in (0, 2):
                at = r * pitch + dw
                a[par, f, r, :, dw * c : (dw + 1) * c] = y[at : at + w, :].astype(BF16)

    def masked(dy, dx, values):
        return jnp.where(exists(dy, dx), values, 0.0)

    SIDE = (-1, 1)

    def build_cached(k):
        par = k % 2

        def body(f, carry):
            build(
                par,
                f,
                lambda r: vc[k, f, r * w : (r + 1) * w, :],
                [lambda i=i: masked(SIDE[i], 0, cr_in[k, i, f]) for i in range(2)],
                [lambda i=i: masked(0, SIDE[i], cc_in[k, i, f]) for i in range(2)],
                [lambda i=i: masked(SIDE[i // 2], SIDE[i % 2], ck_in[k, i, f]) for i in range(4)],
            )
            return carry

        lax.fori_loop(0, cf, body, 0)

    def build_live(k, multiplier, offset):
        par = k % 2

        def act(values):
            return silu(values * multiplier + offset)

        def body(f, carry):
            build(
                par,
                cf + f,
                lambda r: act(v[f, r * w : (r + 1) * w, :]),
                [lambda i=i: masked(SIDE[i], 0, act(lr_in[k, i, f])) for i in range(2)],
                [lambda i=i: masked(0, SIDE[i], act(lc_in[k, i, f])) for i in range(2)],
                [
                    lambda i=i: masked(SIDE[i // 2], SIDE[i % 2], act(lk_in[k, i, f]))
                    for i in range(4)
                ],
            )
            return carry

        lax.fori_loop(0, fr, body, 0)

    def product(k, first, low, high, block):
        par = k % 2
        pieces = []
        for f in range(low, high):
            for dh in range(3):
                piece = a[par, first + f, pl.ds(block * ROW_BLOCK + dh, ROW_BLOCK)]
                pieces.append(piece.reshape(ROW_BLOCK * w, 3 * c))
        left = jnp.concatenate(pieces, axis=1)
        right = t[k, low:high].reshape((high - low) * 9 * c, 2 * c)
        return jnp.dot(left, right, preferred_element_type=F32)

    blocks = h // ROW_BLOCK
    cells = ROW_BLOCK * w

    def conv_cached(k):
        def body(block, carry):
            acc[pl.ds(pl.multiple_of(block * cells, cells), cells), :] = product(k, 0, 0, cf, block)
            return carry

        lax.fori_loop(0, blocks, body, 0)

    def conv_live(k):
        bias_row = bias[k : k + 1, :]
        zero = jnp.zeros((8, c), F32)
        carry = (zero, zero)
        for pair in range(fr // 2):

            def body(block, carry, pair=pair):
                sums, squares = carry
                span = pl.ds(pl.multiple_of(block * cells, cells), cells)
                if pair == 0:
                    both = product(k, 0, cf, cf + 2, block) + acc[span, :]
                else:
                    both = product(k, 2 * pair, 0, 4, block)
                for half in range(2):
                    f = 2 * pair + half
                    result = both[:, half * c : (half + 1) * c] + bias_row
                    if k % 2:
                        rounded = (x[f, span, :].astype(F32) + result).astype(BF16)
                        x[f, span, :] = rounded
                        result = rounded.astype(F32)
                    if k < convs - 1:
                        v[f, span, :] = result
                        slabs = result.reshape(cells // 8, 8, c)
                        sums = sums + jnp.sum(slabs, axis=0)
                        squares = squares + jnp.sum(slabs * slabs, axis=0)
                return sums, squares

            carry = lax.fori_loop(0, blocks, body, carry)
            if k == convs - 1:
                out_copy(pair).start()
        return carry

    def out_copy(pair):
        span = pl.ds(2 * pair, 2)
        return pltpu.make_async_copy(x.at[span], encoded.at[span], out_sem.at[pair])

    def kept_copy(k):
        return pltpu.make_async_copy(
            a.at[k % 2, pl.ds(fr, cf), pl.ds(1, h), :, pl.ds(c, c)], kept.at[:, k], kept_sem.at[k]
        )

    load_x.wait()

    def widen(f, carry):
        sums, squares = carry
        values = x[f].astype(F32)
        v[f] = values
        slabs = values.reshape(h * w // 8, 8, c)
        return sums + jnp.sum(slabs, axis=0), squares + jnp.sum(slabs * slabs, axis=0)

    zero = jnp.zeros((8, c), F32)
    carry = lax.fori_loop(0, fr, widen, (zero, zero))
    pl.semaphore_wait(barrier, peers - 1)
    send_stats(0, *carry)
    send_halo(True, 0)
    load_c.wait()
    for k in range(convs):

        def widen_cache(f, carry, k=k):
            vc[k, f] = cb[f, k].astype(F32)
            return carry

        lax.fori_loop(0, cf, widen_cache, 0)
        send_halo(False, k)

    for k in range(convs):
        if k >= 2:
            kept_copy(k - 2).wait()
        wait_halo(False, k)
        build_cached(k)
        for copy in weight_copies(k):
            copy.wait()
        conv_cached(k)
        multiplier, offset = wait_stats(k)
        wait_halo(True, k)
        build_live(k, multiplier, offset)
        kept_copy(k).start()
        wait_sent(True, k)
        carry = conv_live(k)
        if k < convs - 1:
            send_stats(k + 1, *carry)
            send_halo(True, k + 1)

    for k in range(convs):
        wait_sent(False, k)
        for number in range(peers - 1):
            stat_copy(k, number, me).wait_send()
    for k in range(max(convs - 2, 0), convs):
        kept_copy(k).wait()
    for pair in range(fr // 2):
        out_copy(pair).wait()


def local(nh, nw, frames, caches, conv_weights, conv_bias, norm_gain, norm_shift):
    fr, h, w, c = frames.shape
    cf, convs = caches.shape[:2]
    dims = (nh, nw, fr, cf, convs, h, w, c)
    peers = nh * nw
    vmem = pltpu.VMEM
    dma = pltpu.SemaphoreType.DMA
    scratch = [
        vmem((fr, h * w, c), BF16),
        vmem((cf, convs, h * w, c), BF16),
        vmem((fr, h * w, c), F32),
        vmem((convs, cf, h * w, c), F32),
        vmem((2, fr + cf, h + 2, w, 3 * c), BF16),
        vmem((convs, 4, 3, 3 * c, 2 * c), BF16),
        vmem((h * w, 2 * c), F32),
        vmem(((h + 2) * (w + 8), c), F32),
        vmem((convs, 2, c), F32),
        vmem((convs, peers, 2, c), F32),
    ]
    for nf, sent in ((fr, True), (cf, True)):
        scratch += [
            vmem((convs, 2, nf, h, c), F32),
            vmem((convs, 4, nf, 1, c), F32),
            vmem((convs, 2, nf, w, c), F32),
            vmem((convs, 2, nf, h, c), F32),
            vmem((convs, 4, nf, 1, c), F32),
        ]
    scratch += [
        dma((2,)),
        dma((convs, 6)),
        dma((convs,)),
        dma((fr // 2,)),
        dma((convs, peers - 1)),
        dma((convs, peers)),
        dma((2 * convs, 8)),
        dma((2 * convs, 8)),
    ]
    anywhere = pl.BlockSpec(memory_space=pl.ANY)
    inside = pl.BlockSpec(memory_space=pltpu.VMEM)
    encoded, kept = pl.pallas_call(
        functools.partial(kernel, dims),
        out_shape=(
            jax.ShapeDtypeStruct((fr, h * w, c), BF16),
            jax.ShapeDtypeStruct(caches.shape, BF16),
        ),
        in_specs=[anywhere] * 3 + [inside] * 3,
        out_specs=(anywhere, anywhere),
        scratch_shapes=scratch,
        compiler_params=pltpu.CompilerParams(
            collective_id=0, has_side_effects=True, vmem_limit_bytes=56 * 1024 * 1024
        ),
    )(
        frames.reshape(fr, h * w, c),
        caches.reshape(cf, convs, h * w, c),
        conv_weights.reshape(convs, 3, 3, 3 * c, c),
        conv_bias,
        norm_gain,
        norm_shift,
    )
    return encoded.reshape(frames.shape), kept


def solution(mesh):
    return jax.shard_map(
        functools.partial(local, mesh.shape["ha"], mesh.shape["wa"]),
        mesh=mesh,
        in_specs=(
            P("clip", "ha", "wa", None),
            P("clip", None, "ha", "wa", None),
            P(),
            P(),
            P(),
            P(),
        ),
        out_specs=(P("clip", "ha", "wa", None), P("clip", None, "ha", "wa", None)),
        check_vma=False,
    )
```

time: 294 us -> 56.4 us (0.19); the launches traced: 290 us -> 56.2 us
  blocking collectives: 154 us -> 0 us
  Pallas kernels: 0 us -> 52.3 us
  waiting for transfers between devices: 38.2 us -> 0 us
  matrix products: 35.6 us -> 0 us
  starting transfers between devices: 28.9 us -> 0 us
  local copies, waits for them, and re-layouts: 18.7 us -> 3.33 us
  other arithmetic: 13.2 us -> 0 us
    psum x4 -> x0, blocking collectives: 154 us -> none  [group_norm(): group_total, squares = lax.psum((local_sums, local_squares), ('ha', 'wa'))]
    pallas_call x0 -> x1, Pallas kernels: none -> 52.3 us  [local(): pl.pallas_call(functools.partial(kernel, dims), out_shape=(jax.ShapeDtype...]
    ppermute x16 -> x0, waiting for transfers between devices: 38.2 us -> none  [the longest x8 35.8 us: with_halo(): lax.ppermute(head, axis, [((i + 1) % count, i) for i in range(ends)])]
    conv_general_dilated x4 -> x0, matrix products: 35.6 us -> none  [run_conv(): lax.conv_general_dilated(padded[None], kernel, (1, 1, 1), 'VALID', dimens...]
    ppermute x16 -> x0, starting transfers between devices: 28.9 us -> none  [the longest x8 17.4 us: with_halo(): lax.ppermute(tail, axis, [(i, (i + 1) % count) for i in range(ends)])]
    conv_general_dilated x12 -> x0, local copies, waits for them, and re-layouts: 4.56 us -> none  [run_conv(): lax.conv_general_dilated(padded[None], kernel, (1, 1, 1), 'VALID', dimens...]
    reduce_sum x12 -> x0, other arithmetic: 3.77 us -> none  [the longest x8 3.32 us: group_norm(): jnp.sum(interior, axis=(0, 1, 2)).reshape(groups, per_group).sum(axis=1)]
    broadcast_in_dim x4 -> x0, other arithmetic: 3.62 us -> none  [run_conv(): padded[None]]
  transfers between devices with their start and end apart: 16 -> 0, of which waited for: 12 -> 0; matrix products, arithmetic and copies ran while one was open for 2% -> 0% of each run, Pallas kernels for 0% -> 0%
where the time goes in v1:
time: 56.4 us; the launch traced here: 56.2 us
  Pallas kernels  52.3 us (93%)
  local copies, waits for them, and re-layouts  3.33 us (6%)
  between operations  0.65 us (1%)
    pallas_call x1, Pallas kernels, local(): pl.pallas_call(functools.partial(kernel, dims), out_shape=(jax.ShapeDtype...  52.3 us
    unnamed x4, local copies, waits for them, and re-layouts  3.33 us

profile of v1, /device:TPU:0, one launch (start us, length us, event | category | flops | bytes accessed | tf_op | source)
XLA Modules:
  0.0 56.2 jit_solution(5973097546771981750)
XLA Ops:
  0.6 52.3 %shard_map.77 = (bf16[4,768,128]{2,1,0:T(8,128)(2,1)}, bf16[2,4,24,32,128]{4,3,2,1,0:T(8,128)(2,1)}) custom-call(bf16[4,768,128]{2,1,0:T(8,128)(2,1)} %bitcast.6, bf16[2,4,768,128]{3,2,1,0:T(8,128)(2,1)} %bitcast.5, bf16[4,3,3,384,128]{4,3,2,1,0:T(8,128)(2,1)} %bitcast.4, f32[4,128]{1,0:T(4,128)} %refs_3_.1, f32[4,128]{1,0:T(4,128)} %refs_4_.1, f32[4,128]{1,0:T(4,128)} %refs_5_.1), custom_call_target="tpu_custom_call" | custom-call | tf_op jit(solution)/shard_map/pallas_call | solution.py:399
  52.9 0.0 copy-start
  52.9 2.2 %copy.10 = bf16[4,24,32,128]{3,2,1,0:T(8,128)(2,1)} copy(bf16[4,24,32,128]{3,2,1,0:T(8,128)(2,1)} %bitcast.7) | data formatting | bytes 1572864
  55.1 0.0 copy-done
  55.1 1.1 %copy.11 = bf16[2,4,24,32,128]{4,3,2,1,0:T(8,128)(2,1)} copy(bf16[2,4,24,32,128]{4,3,2,1,0:T(8,128)(2,1)S(1)} %copy-done) | data formatting | bytes 3145728
Async XLA Ops:
  52.9 2.2 %copy-start = (bf16[2,4,24,32,128]{4,3,2,1,0:T(8,128)(2,1)S(1)}, bf16[2,4,24,32,128]{4,3,2,1,0:T(8,128)(2,1)}, u32[]{:S(2)}) copy-start(bf16[2,4,24,32,128]{4,3,2,1,0:T(8,128)(2,1)} %get-tuple-element.9) | copy-start | bytes 4718596

commit v2 on v1

--- a/solution.py
+++ b/solution.py
@@ -12,7 +12,7 @@
 MESH = pl.DeviceIdType.MESH
 F32 = jnp.float32
 BF16 = jnp.bfloat16
-ROW_BLOCK = 8
+ROW_BLOCK = 12
 DIRECTIONS = [(dy, dx) for dy in (-1, 0, 1) for dx in (-1, 0, 1) if (dy, dx) != (0, 0)]
 
 
@@ -20,8 +20,8 @@
     (frames, caches, weights, bias, gain, shift, encoded, kept,
      x, cb, v, vc, a, t, acc, y,
      s_out, s_in,
-     lc_out, lk_out, lr_in, lc_in, lk_in,
-     cc_out, ck_out, cr_in, cc_in, ck_in,
+     lr_out, lc_out, lk_out, lr_in, lc_in, lk_in,
+     cr_out, cc_out, ck_out, cr_in, cc_in, ck_in,
      load_sem, weight_sem, kept_sem, out_sem,
      stat_send, stat_recv, halo_send, halo_recv) = refs
     nh, nw, fr, cf, convs, h, w, c = dims
@@ -58,9 +58,8 @@
                 )
         return copies
 
-    for k in range(convs):
-        for copy in weight_copies(k):
-            copy.start()
+    for copy in weight_copies(0):
+        copy.start()
 
     def zero_weights(k, carry):
         t[k, 3, :, :, 0:c] = jnp.zeros((3, 3 * c, c), BF16)
@@ -77,22 +76,24 @@
             conds.append(wa > 0 if dx < 0 else wa < nw - 1)
         return conds[0] if len(conds) == 1 else jnp.logical_and(*conds)
 
-    def halo_copy(live, k, dy, dx, towards):
-        e = k if live else convs + k
-        field = v if live else vc.at[k]
-        rows_in = lr_in if live else cr_in
+    parts = fr // 2
+
+    def halo_copy(live, k, part, dy, dx, towards):
+        e = k * parts + part if live else convs * parts + k
+        span = pl.ds(2 * part, 2) if live else pl.ds(0, cf)
+        rows_out, rows_in = (lr_out, lr_in) if live else (cr_out, cr_in)
         cols_out, cols_in = (lc_out, lc_in) if live else (cc_out, cc_in)
         ends_out, ends_in = (lk_out, lk_in) if live else (ck_out, ck_in)
         if dx == 0:
-            src = field.at[:, pl.ds(0 if dy < 0 else (h - 1) * w, w), :]
-            dst = rows_in.at[k, int(dy < 0)]
+            src = rows_out.at[k, int(dy > 0), span]
+            dst = rows_in.at[k, int(dy < 0), span]
         elif dy == 0:
-            src = cols_out.at[k, int(dx > 0)]
-            dst = cols_in.at[k, int(dx < 0)]
+            src = cols_out.at[k, int(dx > 0), span]
+            dst = cols_in.at[k, int(dx < 0), span]
         else:
             index = int(dy > 0) * 2 + int(dx > 0)
-            src = ends_out.at[k, index]
-            dst = ends_in.at[k, 3 - index]
+            src = ends_out.at[k, index, span]
+            dst = ends_in.at[k, 3 - index, span]
         d = DIRECTIONS.index((dy, dx))
         back = DIRECTIONS.index((-dy, -dx))
         return pltpu.make_async_remote_copy(
@@ -104,39 +105,44 @@
             device_id_type=MESH,
         )
 
-    def pack_edges(live, k):
+    def pack_edges(live, k, part):
         field = v if live else vc.at[k]
+        rows_out = lr_out if live else cr_out
         cols_out = lc_out if live else cc_out
         ends_out = lk_out if live else ck_out
-        for f in range(fr if live else cf):
+        for f in range(2 * part, 2 * part + 2) if live else range(cf):
             for side in range(2):
                 first = side * (w - 1)
-                cols_out[k, side, f] = field[f, pl.ds(first, h, stride=w), :]
+                top = side * (h - 1) * w
+                rows_out[k, side, f] = field[f, top : top + w, :].astype(BF16)
+                cols_out[k, side, f] = field[f, pl.ds(first, h, stride=w), :].astype(BF16)
                 for low in range(2):
                     row = low * (h - 1) * w + first
                     ends_out[k, low * 2 + side, f] = field[f, row : row + 1, :]
 
-    def send_halo(live, k):
-        pack_edges(live, k)
+    def send_halo(live, k, part):
+        pack_edges(live, k, part)
         for dy, dx in DIRECTIONS:
 
             @pl.when(exists(dy, dx))
             def _():
-                halo_copy(live, k, dy, dx, 1).start()
+                halo_copy(live, k, part, dy, dx, 1).start()
 
     def wait_halo(live, k):
         for dy, dx in DIRECTIONS:
 
             @pl.when(exists(dy, dx))
             def _():
-                halo_copy(live, k, -dy, -dx, -1).wait_recv()
+                for part in range(parts if live else 1):
+                    halo_copy(live, k, part, -dy, -dx, -1).wait_recv()
 
     def wait_sent(live, k):
         for dy, dx in DIRECTIONS:
 
             @pl.when(exists(dy, dx))
             def _():
-                halo_copy(live, k, dy, dx, 1).wait_send()
+                for part in range(parts if live else 1):
+                    halo_copy(live, k, part, dy, dx, 1).wait_send()
 
     def stat_copy(k, number, sender):
         ph, pw = others[number]
@@ -213,8 +219,8 @@
                 par,
                 f,
                 lambda r: vc[k, f, r * w : (r + 1) * w, :],
-                [lambda i=i: masked(SIDE[i], 0, cr_in[k, i, f]) for i in range(2)],
-                [lambda i=i: masked(0, SIDE[i], cc_in[k, i, f]) for i in range(2)],
+                [lambda i=i: masked(SIDE[i], 0, cr_in[k, i, f].astype(F32)) for i in range(2)],
+                [lambda i=i: masked(0, SIDE[i], cc_in[k, i, f].astype(F32)) for i in range(2)],
                 [lambda i=i: masked(SIDE[i // 2], SIDE[i % 2], ck_in[k, i, f]) for i in range(4)],
             )
             return carry
@@ -232,8 +238,8 @@
                 par,
                 cf + f,
                 lambda r: act(v[f, r * w : (r + 1) * w, :]),
-                [lambda i=i: masked(SIDE[i], 0, act(lr_in[k, i, f])) for i in range(2)],
-                [lambda i=i: masked(0, SIDE[i], act(lc_in[k, i, f])) for i in range(2)],
+                [lambda i=i: masked(SIDE[i], 0, act(lr_in[k, i, f].astype(F32))) for i in range(2)],
+                [lambda i=i: masked(0, SIDE[i], act(lc_in[k, i, f].astype(F32))) for i in range(2)],
                 [
                     lambda i=i: masked(SIDE[i // 2], SIDE[i % 2], act(lk_in[k, i, f]))
                     for i in range(4)
@@ -294,6 +300,8 @@
             carry = lax.fori_loop(0, blocks, body, carry)
             if k == convs - 1:
                 out_copy(pair).start()
+            elif pair < parts - 1:
+                send_halo(True, k + 1, pair)
         return carry
 
     def out_copy(pair):
@@ -304,6 +312,12 @@
         return pltpu.make_async_copy(
             a.at[k % 2, pl.ds(fr, cf), pl.ds(1, h), :, pl.ds(c, c)], kept.at[:, k], kept_sem.at[k]
         )
+
+    def settle(k):
+        wait_sent(True, k)
+        wait_sent(False, k)
+        for number in range(peers - 1):
+            stat_copy(k, number, me).wait_send()
 
     load_x.wait()
 
@@ -318,17 +332,19 @@
     carry = lax.fori_loop(0, fr, widen, (zero, zero))
     pl.semaphore_wait(barrier, peers - 1)
     send_stats(0, *carry)
-    send_halo(True, 0)
-    load_c.wait()
-    for k in range(convs):
-
-        def widen_cache(f, carry, k=k):
+    for part in range(parts):
+        send_halo(True, 0, part)
+
+    def send_cached(k):
+        def widen_cache(f, carry):
             vc[k, f] = cb[f, k].astype(F32)
             return carry
 
         lax.fori_loop(0, cf, widen_cache, 0)
-        send_halo(False, k)
-
+        send_halo(False, k, 0)
+
+    load_c.wait()
+    send_cached(0)
     for k in range(convs):
         if k >= 2:
             kept_copy(k - 2).wait()
@@ -337,23 +353,25 @@
         for copy in weight_copies(k):
             copy.wait()
         conv_cached(k)
+        if k < convs - 1:
+            for copy in weight_copies(k + 1):
+                copy.start()
+            send_cached(k + 1)
+        if k:
+            settle(k - 1)
         multiplier, offset = wait_stats(k)
         wait_halo(True, k)
         build_live(k, multiplier, offset)
         kept_copy(k).start()
-        wait_sent(True, k)
         carry = conv_live(k)
         if k < convs - 1:
             send_stats(k + 1, *carry)
-            send_halo(True, k + 1)
-
-    for k in range(convs):
-        wait_sent(False, k)
-        for number in range(peers - 1):
-            stat_copy(k, number, me).wait_send()
+            send_halo(True, k + 1, parts - 1)
+
+    settle(convs - 1)
     for k in range(max(convs - 2, 0), convs):
         kept_copy(k).wait()
-    for pair in range(fr // 2):
+    for pair in range(parts):
         out_copy(pair).wait()
 
 
@@ -376,12 +394,13 @@
         vmem((convs, 2, c), F32),
         vmem((convs, peers, 2, c), F32),
     ]
-    for nf, sent in ((fr, True), (cf, True)):
+    for nf in (fr, cf):
         scratch += [
-            vmem((convs, 2, nf, h, c), F32),
+            vmem((convs, 2, nf, w, c), BF16),
+            vmem((convs, 2, nf, h, c), BF16),
             vmem((convs, 4, nf, 1, c), F32),
-            vmem((convs, 2, nf, w, c), F32),
-            vmem((convs, 2, nf, h, c), F32),
+            vmem((convs, 2, nf, w, c), BF16),
+            vmem((convs, 2, nf, h, c), BF16),
             vmem((convs, 4, nf, 1, c), F32),
         ]
     scratch += [
@@ -391,8 +410,8 @@
         dma((fr // 2,)),
         dma((convs, peers - 1)),
         dma((convs, peers)),
-        dma((2 * convs, 8)),
-        dma((2 * convs, 8)),
+        dma((convs * (fr // 2 + 1), 8)),
+        dma((convs * (fr // 2 + 1), 8)),
     ]
     anywhere = pl.BlockSpec(memory_space=pl.ANY)
     inside = pl.BlockSpec(memory_space=pltpu.VMEM)

time: 56.4 us -> 51.1 us (0.906)
  Pallas kernels: 52.3 us -> 47 us
    pallas_call x1, Pallas kernels: 52.3 us -> 47 us  [local(): pl.pallas_call(functools.partial(kernel, dims), out_shape=(jax.ShapeDtype...]
where the time goes in v2:
time: 51.1 us; the launch traced here: 50.9 us
  Pallas kernels  47 us (92%)
  local copies, waits for them, and re-layouts  3.33 us (7%)
  between operations  0.65 us (1%)
    pallas_call x1, Pallas kernels, local(): pl.pallas_call(functools.partial(kernel, dims), out_shape=(jax.ShapeDtype...  47 us
    unnamed x4, local copies, waits for them, and re-layouts  3.33 us

profile of v2, /device:TPU:0, one launch (start us, length us, event | category | flops | bytes accessed | tf_op | source)
XLA Modules:
  0.0 50.9 jit_solution(17239416024005400564)
XLA Ops:
  0.6 47.0 %shard_map.77 = (bf16[4,768,128]{2,1,0:T(8,128)(2,1)}, bf16[2,4,24,32,128]{4,3,2,1,0:T(8,128)(2,1)}) custom-call(bf16[4,768,128]{2,1,0:T(8,128)(2,1)} %bitcast.6, bf16[2,4,768,128]{3,2,1,0:T(8,128)(2,1)} %bitcast.5, bf16[4,3,3,384,128]{4,3,2,1,0:T(8,128)(2,1)} %bitcast.4, f32[4,128]{1,0:T(4,128)} %refs_3_.1, f32[4,128]{1,0:T(4,128)} %refs_4_.1, f32[4,128]{1,0:T(4,128)} %refs_5_.1), custom_call_target="tpu_custom_call" | custom-call | tf_op jit(solution)/shard_map/pallas_call | solution.py:418
  47.6 0.0 copy-start
  47.6 2.2 %copy.10 = bf16[4,24,32,128]{3,2,1,0:T(8,128)(2,1)} copy(bf16[4,24,32,128]{3,2,1,0:T(8,128)(2,1)} %bitcast.7) | data formatting | bytes 1572864
  49.8 0.0 copy-done
  49.8 1.1 %copy.11 = bf16[2,4,24,32,128]{4,3,2,1,0:T(8,128)(2,1)} copy(bf16[2,4,24,32,128]{4,3,2,1,0:T(8,128)(2,1)S(1)} %copy-done) | data formatting | bytes 3145728
Async XLA Ops:
  47.6 2.2 %copy-start = (bf16[2,4,24,32,128]{4,3,2,1,0:T(8,128)(2,1)S(1)}, bf16[2,4,24,32,128]{4,3,2,1,0:T(8,128)(2,1)}, u32[]{:S(2)}) copy-start(bf16[2,4,24,32,128]{4,3,2,1,0:T(8,128)(2,1)} %get-tuple-element.9) | copy-start | bytes 4718596
